TPU v7x, 256 devices: a whole 4x4x8 slice. The times are simulated.
256 devices in a mesh: crop: 4 (over z_hi, core), row: 64 (over y, x, z_lo).
Axes of the slice: x: 4, y: 4, z: 8 (z_hi: 2, z_lo: 4; z = z_hi * 4 + z_lo), core: 2. Of those that a mesh axis runs over, the one named last changes fastest.
Arguments:
- pair: bfloat16 [4, 512, 512, 128], P('crop', 'row'), may hold values from -6 to 6
- cotangent: bfloat16 [4, 512, 512, 128], P('crop', 'row'), may hold values from -6 to 6
- lengths: int32 [4], P('crop'), may hold values from 256 to 512
- proj_weight: bfloat16 [128, 640], replicated, may hold values from -0.5 to 0.5
- out_weight: bfloat16 [128, 128], replicated, may hold values from -0.5 to 0.5
- up_weight: bfloat16 [128, 512], replicated, may hold values from -0.5 to 0.5
- down_weight: bfloat16 [512, 128], replicated, may hold values from -0.25 to 0.25
- norm_gain: float32 [3, 128], replicated, may hold values from 0.1 to 1.9
- norm_bias: float32 [3, 128], replicated, may hold values from -3 to 3
Outputs:
- grad_pair: bfloat16 [4, 512, 512, 128], P('crop', 'row')
- grad_proj: float32 [128, 640], replicated
- grad_out: float32 [128, 128], replicated
- grad_up: float32 [128, 512], replicated
- grad_down: float32 [512, 128], replicated
- grad_gain: float32 [3, 128], replicated
- grad_bias: float32 [3, 128], replicated
Inputs may be any that keep to these rules, and one draw needn't show every extreme that they name: lengths[s] residues of crop s are present; the rest are masked.
All inputs are finite; a program needn't handle non-finite values.
Results may differ from a plain program's by a relative error of at most 0.009.
Values may be sent and summed in bfloat16 or wider, within the bound.
A program may use at most 128 MiB of HBM per device.

v0:
```python
import jax
import jax.numpy as jnp
from jax import lax
from jax.sharding import PartitionSpec as P

EPSILON = 1e-05


def side_by_side(arrays, axis, split_dim, concat_dim, along):
    widths = [a.shape[along] for a in arrays]
    both = jnp.concatenate(arrays, axis=along)
    filled = lax.all_to_all(both, axis, split_axis=split_dim, concat_axis=concat_dim, tiled=True)
    return tuple(jnp.split(filled, [sum(widths[:k]) for k in range(1, len(widths))], axis=along))


def together(arrays, axis):
    vector, at, outs = (jnp.concatenate([a.reshape(-1) for a in arrays]), 0, [])
    total = lax.psum(vector, axis)
    for a in arrays:
        outs.append(total[at : at + a.size].reshape(a.shape))
        at += a.size
    return tuple(outs)


def for_sending(x):
    return jax.tree.map(lambda a: a.astype(jnp.bfloat16) if a.dtype == jnp.float32 else a, x)


def contract(pattern, left_side, right_side):
    return jnp.einsum(pattern, left_side, right_side, preferred_element_type=jnp.float32)


def norm_forward(values, gain_vec, bias_vec, norm_axis):
    center = values - jnp.mean(values, axis=norm_axis, keepdims=True)
    inv_std = lax.rsqrt(jnp.mean(center * center, axis=norm_axis, keepdims=True) + EPSILON)
    normed = center * inv_std
    return (normed, inv_std, normed * gain_vec + bias_vec)


def norm_backward(upstream, normed, inv_std, gain_vec, norm_axis, others):
    grad_gain = jnp.sum(upstream * normed, axis=others)
    grad_bias = jnp.sum(upstream, axis=others)
    scaled = upstream * gain_vec
    result = inv_std * (
        scaled
        - jnp.mean(scaled, axis=norm_axis, keepdims=True)
        - normed * jnp.mean(scaled * normed, axis=norm_axis, keepdims=True)
    )
    return (result, grad_gain, grad_bias)


def enter_rows(pair_rows, row_keep, col_keep, proj_weight, norm_gain, norm_bias):
    channels = pair_rows.shape[2]
    normed_in, inv_in, scaled_in = norm_forward(
        pair_rows.astype(jnp.float32), norm_gain[0], norm_bias[0], 2
    )
    input_bf = scaled_in.astype(jnp.bfloat16)
    factor_pre = contract("rld,de->erl", input_bf, proj_weight[:, : 4 * channels])
    gate_pre = contract("rld,de->rle", input_bf, proj_weight[:, 4 * channels :])
    keep_both = row_keep[:, None] * col_keep[None, :]
    left_bf = (
        jax.nn.sigmoid(factor_pre[:channels]) * factor_pre[channels : 2 * channels] * keep_both
    ).astype(jnp.bfloat16)
    right_bf = (
        jax.nn.sigmoid(factor_pre[2 * channels : 3 * channels])
        * factor_pre[3 * channels :]
        * keep_both
    ).astype(jnp.bfloat16)
    return (input_bf, normed_in, inv_in, factor_pre, gate_pre, keep_both, left_bf, right_bf)


def middle_rows(
    pair_rows,
    cot_rows,
    product_bf,
    gate_pre,
    out_weight,
    up_weight,
    down_weight,
    norm_gain,
    norm_bias,
):
    prod_normed, prod_inv, prod_scaled = norm_forward(
        product_bf.astype(jnp.float32), norm_gain[1][:, None, None], norm_bias[1][:, None, None], 0
    )
    prod_norm_bf = prod_scaled.astype(jnp.bfloat16)
    update = contract("crj,cd->rjd", prod_norm_bf, out_weight)
    gate_sig = jax.nn.sigmoid(gate_pre)
    first_bf = (pair_rows.astype(jnp.float32) + gate_sig * update).astype(jnp.bfloat16)
    tran_normed, tran_inv, tran_scaled = norm_forward(
        first_bf.astype(jnp.float32), norm_gain[2], norm_bias[2], 2
    )
    tran_bf = tran_scaled.astype(jnp.bfloat16)
    hidden_pre = contract("rld,dh->rlh", tran_bf, up_weight)
    hidden_sig = jax.nn.sigmoid(hidden_pre)
    hidden_bf = (hidden_pre * hidden_sig).astype(jnp.bfloat16)
    grad_down = contract("rlh,rld->hd", hidden_bf, cot_rows)
    hidden_grad_bf = (
        contract("rld,hd->rlh", cot_rows, down_weight)
        * hidden_sig
        * (1.0 + hidden_pre * (1.0 - hidden_sig))
    ).astype(jnp.bfloat16)
    grad_up = contract("rld,rlh->dh", tran_bf, hidden_grad_bf)
    tran_grad = contract("rlh,dh->rld", hidden_grad_bf, up_weight)
    first_grad, gain_tran, bias_tran = norm_backward(
        tran_grad, tran_normed, tran_inv, norm_gain[2], 2, (0, 1)
    )
    first_grad = first_grad + cot_rows.astype(jnp.float32)
    update_grad_bf = (first_grad * gate_sig).astype(jnp.bfloat16)
    gate_grad_bf = (first_grad * update * gate_sig * (1.0 - gate_sig)).astype(jnp.bfloat16)
    grad_out = contract("crj,rjd->cd", prod_norm_bf, update_grad_bf)
    norm_grad = contract("rjd,cd->crj", update_grad_bf, out_weight)
    prod_grad, gain_prod, bias_prod = norm_backward(
        norm_grad, prod_normed, prod_inv, norm_gain[1][:, None, None], 0, (1, 2)
    )
    return (
        prod_grad.astype(jnp.bfloat16),
        first_grad,
        gate_grad_bf,
        grad_out,
        grad_up,
        grad_down,
        gain_prod,
        bias_prod,
        gain_tran,
        bias_tran,
    )


def leave_rows(
    left_grad,
    right_grad,
    factor_pre,
    keep_both,
    gate_grad_bf,
    input_bf,
    normed_in,
    inv_in,
    first_grad,
    proj_weight,
    norm_gain,
):
    channels = gate_grad_bf.shape[2]
    sig_left = jax.nn.sigmoid(factor_pre[:channels])
    lin_left = factor_pre[channels : 2 * channels]
    sig_right = jax.nn.sigmoid(factor_pre[2 * channels : 3 * channels])
    lin_right = factor_pre[3 * channels :]
    masked_left = left_grad.astype(jnp.float32) * keep_both
    masked_right = right_grad.astype(jnp.float32) * keep_both
    factor_grad = jnp.concatenate(
        [
            masked_left * lin_left * sig_left * (1.0 - sig_left),
            masked_left * sig_left,
            masked_right * lin_right * sig_right * (1.0 - sig_right),
            masked_right * sig_right,
        ],
        axis=0,
    ).astype(jnp.bfloat16)
    grad_proj = jnp.concatenate(
        [
            contract("rld,erl->de", input_bf, factor_grad),
            contract("rld,rle->de", input_bf, gate_grad_bf),
        ],
        axis=1,
    )
    input_grad = contract("erl,de->rld", factor_grad, proj_weight[:, : 4 * channels]) + contract(
        "rle,de->rld", gate_grad_bf, proj_weight[:, 4 * channels :]
    )
    pair_grad, gain_in, bias_in = norm_backward(
        input_grad, normed_in, inv_in, norm_gain[0], 2, (0, 1)
    )
    return ((pair_grad + first_grad).astype(jnp.bfloat16), grad_proj, gain_in, bias_in)


def channel_products(left_part, right_part):
    return contract("acik,acjk->acij", left_part, right_part).astype(jnp.bfloat16)


def channel_grads(grad_part, left_part, right_part):
    left_grad = contract("acij,acjk->acik", grad_part, right_part).astype(jnp.bfloat16)
    right_grad = contract("acij,acik->acjk", grad_part, left_part).astype(jnp.bfloat16)
    return (left_grad, right_grad)


def local(
    pair, cotangent, lengths, proj_weight, out_weight, up_weight, down_weight, norm_gain, norm_bias
):
    pair_rows = pair[0]
    cot_rows = cotangent[0]
    rows_here, length_all, channels = pair_rows.shape
    groups = lax.axis_size("row")
    per_group = channels // groups
    first_row = lax.axis_index("row") * rows_here
    row_keep = (first_row + jnp.arange(rows_here, dtype=jnp.int32) < lengths[0]).astype(jnp.float32)
    col_keep = (jnp.arange(length_all, dtype=jnp.int32) < lengths[0]).astype(jnp.float32)
    entered = enter_rows(pair_rows, row_keep, col_keep, proj_weight, norm_gain, norm_bias)
    input_bf, normed_in, inv_in, factor_pre, gate_pre, keep_both, left_bf, right_bf = entered
    left_split = left_bf.reshape(groups, per_group, rows_here, length_all)
    right_split = right_bf.reshape(groups, per_group, rows_here, length_all)
    left_owned, right_owned = side_by_side((left_split, right_split), "row", 0, 2, 1)
    product_owned = channel_products(left_owned, right_owned)
    product_split = lax.all_to_all(product_owned, "row", split_axis=2, concat_axis=0, tiled=True)
    product_bf = product_split.reshape(channels, rows_here, length_all)
    middle = middle_rows(
        pair_rows,
        cot_rows,
        product_bf,
        gate_pre,
        out_weight,
        up_weight,
        down_weight,
        norm_gain,
        norm_bias,
    )
    (
        prod_grad_bf,
        first_grad,
        gate_grad_bf,
        grad_out,
        grad_up,
        grad_down,
        gain_prod,
        bias_prod,
        gain_tran,
        bias_tran,
    ) = middle
    summed_up, summed_down = together((grad_up, grad_down), ("crop", "row"))
    grad_split = prod_grad_bf.reshape(groups, per_group, rows_here, length_all)
    grad_owned = lax.all_to_all(grad_split, "row", split_axis=0, concat_axis=2, tiled=True)
    left_home, right_home = lax.all_to_all(
        for_sending(channel_grads(grad_owned, left_owned, right_owned)),
        "row",
        split_axis=2,
        concat_axis=0,
        tiled=True,
    )
    left_grad = left_home.reshape(channels, rows_here, length_all)
    right_grad = right_home.reshape(channels, rows_here, length_all)
    pair_grad, grad_proj, gain_in, bias_in = leave_rows(
        left_grad,
        right_grad,
        factor_pre,
        keep_both,
        gate_grad_bf,
        input_bf,
        normed_in,
        inv_in,
        first_grad,
        proj_weight,
        norm_gain,
    )
    gain_all = jnp.stack([gain_in, gain_prod, gain_tran])
    bias_all = jnp.stack([bias_in, bias_prod, bias_tran])
    summed_proj, summed_out, summed_gain, summed_bias = lax.psum(
        (grad_proj, grad_out, gain_all, bias_all), ("crop", "row")
    )
    factor = 1.0 / (rows_here * groups)
    return (
        pair_grad[None],
        summed_proj * factor,
        summed_out * factor,
        summed_up * factor,
        summed_down * factor,
        summed_gain * factor,
        summed_bias * factor,
    )


def solution(mesh):
    in_specs = (
        P("crop", "row", None, None),
        P("crop", "row", None, None),
        P("crop"),
        P(),
        P(),
        P(),
        P(),
        P(),
        P(),
    )
    out_specs = (P("crop", "row", None, None), P(), P(), P(), P(), P(), P())
    return jax.shard_map(local, mesh=mesh, in_specs=in_specs, out_specs=out_specs, check_vma=False)
```

profile of v0, /device:TPU:1, one launch (start us, length us, event | category | flops | bytes accessed | tf_op | source)
XLA Modules:
  0.0 556.9 jit_solution(11000184731263995300)
XLA Ops:
  7.9 1.5 copy.46
  10.6 1.3 convolution_bitcast_fusion.1
  12.0 1.4 multiply_convert_fusion.11
  13.4 1.8 copy-done.2
  15.2 1.3 reshape.196
  16.5 1.2 reshape.197
  17.9 3.2 pad_maximum_fusion.1
  21.2 1.1 copy.100
  22.3 62.7 %all_to_all.60 = bf16[64,4,8,512]{3,1,2,0:T(4,128)(2,1)S(1)} all-to-all(bf16[64,4,8,512]{3,1,2,0:T(4,128)(2,1)S(1)} %copy.100), channel_id=1, replica_groups=mesh['crop'=4,'row'=64] {'row'}, dimensions={0} | all-to-all | bytes 4194304 | tf_op jit(solution)/shard_map/all_to_all | solution.py:12
  85.5 1.3 copy-done.17
  86.8 0.7 fusion.40
  87.5 2.1 copy.52
  89.7 5.6 all-to-all-start.1
  95.3 1.3 copy.57
  96.6 27.0 %all-to-all-done.1 = bf16[1,2,512,512]{3,1,0,2:T(2,128)(2,1)S(1)} async-done(((bf16[1,2,512,512]{3,1,0,2:T(2,128)(2,1)}), bf16[1,2,512,512]{3,1,0,2:T(2,128)(2,1)S(1)}, u32[]{:S(2)}, u32[]{:S(2)}) %all-to-all-start.1) | async-done | bytes 1048608 | tf_op jit(solution)/shard_map/all_to_all | solution.py:202
  123.6 0.8 fusion.75
  124.4 2.1 copy_bitcast_fusion.2
  126.6 1.4 multiply_reduce_fusion.1
  128.0 2.7 reshape.204
  132.1 2.5 convert_reduce_fusion
  135.6 1.4 fusion.56
  137.0 3.4 multiply_convert_fusion.1
  140.5 3.2 fusion.81
  143.7 2.1 copy.60
  145.9 2.8 fusion.20
  148.8 4.7 multiply_convert_fusion.3
  153.5 1.4 fusion.38
  154.9 1.3 copy-done.7
  156.2 1.7 multiply_convert_fusion.8
  157.9 2.3 reshape.200
  160.2 3.4 copy.62
  163.5 5.5 all-to-all-start.2
  169.1 3.3 convolution_bitcast_fusion.2
  172.4 2.4 reduce_sum.178
  174.8 22.4 %all-to-all-done.2 = bf16[64,2,8,512]{3,1,2,0:T(2,128)(2,1)} async-done(((bf16[64,2,8,512]{3,1,2,0:T(2,128)(2,1)}), bf16[64,2,8,512]{3,1,2,0:T(2,128)(2,1)}, u32[]{:S(2)}, u32[]{:S(2)}) %all-to-all-start.2) | async-done | bytes 1048608 | tf_op jit(solution)/shard_map/all_to_all | solution.py:229
  197.2 2.2 fusion.41
  199.4 2.1 copy.64
  201.5 6.1 %all-to-all-start.3 = ((bf16[1,2,512,512]{3,1,0,2:T(2,128)(2,1)}), bf16[1,2,512,512]{3,1,0,2:T(2,128)(2,1)}, u32[]{:S(2)}, u32[]{:S(2)}) async-start(bf16[1,2,512,512]{3,1,0,2:T(2,128)(2,1)} %copy.64), calls=%async_computation.3 | async-start | bytes 2097152 | tf_op jit(solution)/shard_map/all_to_all | solution.py:230
  207.6 2.7 convolution_bitcast_fusion.4
  210.3 1.2 convolution_bitcast_fusion.5
  211.5 6.6 %convolution_bitcast_fusion = f32[65536]{0:T(1024)} fusion(f32[8,512,512]{2,1,0:T(8,128)} %copy-done.11, bf16[1,8,512,128]{3,2,1,0:T(8,128)(2,1)S(1)} %copy-done.21), kind=kOutput, calls=%fused_computation | convolution fusion | flops 547356672 | bytes 9699328 | tf_op jit(solution)/shard_map/rlh,rld->hd/dot_general | solution.py:30
  218.1 2.0 fusion.42
  220.1 2.1 copy.67
  222.3 13.3 %all-to-all-done.3 = bf16[1,2,512,512]{3,1,0,2:T(2,128)(2,1)} async-done(((bf16[1,2,512,512]{3,1,0,2:T(2,128)(2,1)}), bf16[1,2,512,512]{3,1,0,2:T(2,128)(2,1)}, u32[]{:S(2)}, u32[]{:S(2)}) %all-to-all-start.3) | async-done | bytes 1048608 | tf_op jit(solution)/shard_map/all_to_all | solution.py:230
  235.6 5.5 all-to-all-start.4
  241.2 1.8 pad_maximum_fusion.4
  243.0 3.3 copy_bitcast_fusion.1
  246.3 3.8 reshape.205
  250.1 19.1 %all-to-all-done.4 = bf16[1,2,512,512]{3,1,0,2:T(2,128)(2,1)} async-done(((bf16[1,2,512,512]{3,1,0,2:T(2,128)(2,1)}), bf16[1,2,512,512]{3,1,0,2:T(2,128)(2,1)}, u32[]{:S(2)}, u32[]{:S(2)}) %all-to-all-start.4) | async-done | bytes 1048608 | tf_op jit(solution)/shard_map/all_to_all | solution.py:230
  269.1 3.3 copy_bitcast_fusion
  272.4 3.7 reshape.206
  276.1 5.6 %multiply_convert_fusion.7 = (bf16[128,8,512]{2,0,1:T(8,128)(2,1)S(1)}, bf16[128,8,512]{2,0,1:T(8,128)(2,1)S(1)}, bf16[128,8,512]{2,0,1:T(8,128)(2,1)S(1)}, bf16[128,8,512]{2,0,1:T(8,128)(2,1)S(1)}) fusion(f32[512,8,512]{2,0,1:T(8,128)} %copy-done.2, f32[128,8,512]{2,0,1:T(8,128)} %reshape.205, f32[8,512]{1,0:T(8,128)S(1)} %copy-done.31, ...), kind=kLoop, calls=%fused_computation.62 | loop fusion | flops 11534336 | bytes 16793600 | tf_op jit(solution)/shard_map/convert.11
  281.8 1.6 convolution_bitcast_fusion.3
  283.4 0.7 fusion.50
  284.6 2.8 fusion.29
  287.4 0.7 pad_maximum_fusion.5
  288.9 4.7 fusion.47
  293.7 2.3 copy.81
  296.0 75.2 %all-reduce = (f32[3,128]{1,0:T(4,128)S(1)}, f32[3,128]{1,0:T(4,128)S(1)}) all-reduce(f32[3,128]{1,0:T(4,128)S(1)} %pad_maximum_fusion.6, f32[3,128]{1,0:T(4,128)S(1)} %pad_maximum_fusion.7), channel_id=1, replica_groups=mesh['crop'=4,'row'=64] {'crop','row'}, use_global_device_ids=true, to_apply=%region_18.0 | all-reduce | flops 768 | bytes 6144 | tf_op jit(solution)/shard_map/psum | solution.py:254
  372.3 171.8 %all-reduce.4.cloned.1.call-done = (f32[128,640]{1,0:T(8,128)}, f32[128,128]{1,0:T(8,128)}, f32[131072]{0:T(1024)}) async-done(((f32[128,640]{1,0:T(8,128)}, f32[128,128]{1,0:T(8,128)}, f32[131072]{0:T(1024)}), (f32[128,640]{1,0:T(8,128)}, f32[128,128]{1,0:T(8,128)}, f32[131072]{0:T(1024)})) %all-reduce.4.cloned.1.call-update) | async-done | bytes 917520 | tf_op jit(solution)/shard_map/psum | solution.py:254
  544.1 1.7 broadcast_multiply_fusion
  545.9 1.5 broadcast_multiply_fusion.1
  547.3 1.8 fusion.51
  549.1 0.7 mul.346
  (126 shorter events, 6.7 us)
Async XLA Ops:
  7.2 128.4 %copy-start = (bf16[128,512]{1,0:T(8,128)(2,1)S(1)}, bf16[128,512]{1,0:T(8,128)(2,1)}, u32[]{:S(2)}) copy-start(bf16[128,512]{1,0:T(8,128)(2,1)} %param.14) | copy-start | bytes 393220
  7.9 2.1 copy-start.47
  7.9 2.1 copy-start.48
  7.9 2.7 copy-start.28
  9.6 122.3 %copy-start.22 = (f32[8,512]{1,0:T(8,128)}, f32[8,512]{1,0:T(8,128)S(1)}, u32[]{:S(2)}) copy-start(f32[8,512]{1,0:T(8,128)S(1)} %broadcast_multiply_fusion.11) | copy-start | bytes 49156
  10.0 122.0 %copy-start.26 = (f32[8,512]{1,0:T(8,128)}, f32[8,512]{1,0:T(8,128)S(1)}, u32[]{:S(2)}) copy-start(f32[8,512]{1,0:T(8,128)S(1)} %add_rsqrt_fusion.2) | copy-start | bytes 49156
  10.5 120.2 %copy-start.38 = (f32[128]{0:T(128)}, f32[128]{0:T(128)S(1)}, u32[]{:S(2)}) copy-start(f32[128]{0:T(128)S(1)} %get-tuple-element.61) | copy-start | bytes 1540
  10.5 121.5 %copy-start.36 = (f32[128]{0:T(128)}, f32[128]{0:T(128)S(1)}, u32[]{:S(2)}) copy-start(f32[128]{0:T(128)S(1)} %get-tuple-element.62) | copy-start | bytes 1540
  10.5 121.5 %copy-start.40 = (f32[128]{0:T(128)}, f32[128]{0:T(128)S(1)}, u32[]{:S(2)}) copy-start(f32[128]{0:T(128)S(1)} %get-tuple-element.54) | copy-start | bytes 1540
  10.6 1.4 copy-start.30
  12.0 3.2 copy-start.2
  16.5 1.5 copy-start.14
  85.4 1.3 copy-start.17
  87.5 7.7 %copy-start.19 = (bf16[1,8,512,128]{3,2,1,0:T(8,128)(2,1)S(1)}, bf16[1,8,512,128]{3,2,1,0:T(8,128)(2,1)}, u32[]{:S(2)}) copy-start(bf16[1,8,512,128]{3,2,1,0:T(8,128)(2,1)} %param.10) | copy-start | bytes 3145732
  89.7 33.9 %all-to-all-start.1 = ((bf16[1,2,512,512]{3,1,0,2:T(2,128)(2,1)}), bf16[1,2,512,512]{3,1,0,2:T(2,128)(2,1)S(1)}, u32[]{:S(2)}, u32[]{:S(2)}) async-start(bf16[1,2,512,512]{3,1,0,2:T(2,128)(2,1)} %copy.52), calls=%async_computation.1 | async-start | bytes 2097152 | tf_op jit(solution)/shard_map/all_to_all | solution.py:202
  130.7 1.3 copy-start.3
  130.7 0.8 copy-start.32
  131.5 3.1 copy-start.8
  132.0 2.6 copy-start.12
  132.0 3.5 copy-start.34
  132.1 3.5 copy-start.43
  134.6 1.0 copy-start.5
  134.9 34.1 %copy-start.24 = (f32[8,512]{1,0:T(8,128)}, f32[8,512]{1,0:T(8,128)S(1)}, u32[]{:S(2)}) copy-start(f32[8,512]{1,0:T(8,128)S(1)} %add_rsqrt_fusion) | copy-start | bytes 49156
  135.6 1.4 copy-start.20
  135.6 1.4 copy-start.49
  137.0 3.5 copy-start.11
  140.5 3.2 copy-start.13
  143.7 2.2 copy-start.35
  145.9 2.9 copy-start.6
  145.9 2.9 copy-start.9
  148.7 4.7 copy-start.4
  148.8 4.7 copy-start.39
  153.5 1.4 copy-start.10
  154.9 1.3 copy-start.7
  160.2 8.9 %copy-start.44 = (f32[128]{0:T(128)S(1)}, f32[128]{0:T(128)}, u32[]{:S(2)}) copy-start(f32[128]{0:T(128)} %get-tuple-element.53) | copy-start | bytes 1540
  163.5 33.6 %all-to-all-start.2 = ((bf16[64,2,8,512]{3,1,2,0:T(2,128)(2,1)}), bf16[64,2,8,512]{3,1,2,0:T(2,128)(2,1)}, u32[]{:S(2)}, u32[]{:S(2)}) async-start(bf16[64,2,8,512]{3,1,2,0:T(2,128)(2,1)} %copy.62), calls=%async_computation.2 | async-start | bytes 2097152 | tf_op jit(solution)/shard_map/all_to_all | solution.py:229
  201.5 8.8 %copy-start.23 = (f32[8,512]{1,0:T(8,128)S(1)}, f32[8,512]{1,0:T(8,128)}, u32[]{:S(2)}) copy-start(f32[8,512]{1,0:T(8,128)} %copy-done.22) | copy-start | bytes 49156
  201.5 8.8 %copy-start.27 = (f32[8,512]{1,0:T(8,128)S(1)}, f32[8,512]{1,0:T(8,128)}, u32[]{:S(2)}) copy-start(f32[8,512]{1,0:T(8,128)} %copy-done.26) | copy-start | bytes 49156
  201.5 8.8 %copy-start.37 = (f32[128]{0:T(128)S(1)}, f32[128]{0:T(128)}, u32[]{:S(2)}) copy-start(f32[128]{0:T(128)} %copy-done.36) | copy-start | bytes 1540
  201.5 8.8 %copy-start.41 = (f32[128]{0:T(128)S(1)}, f32[128]{0:T(128)}, u32[]{:S(2)}) copy-start(f32[128]{0:T(128)} %copy-done.40) | copy-start | bytes 1540
  201.5 34.1 %all-to-all-start.3 = ((bf16[1,2,512,512]{3,1,0,2:T(2,128)(2,1)}), bf16[1,2,512,512]{3,1,0,2:T(2,128)(2,1)}, u32[]{:S(2)}, u32[]{:S(2)}) async-start(bf16[1,2,512,512]{3,1,0,2:T(2,128)(2,1)} %copy.64), calls=%async_computation.3 | async-start | bytes 2097152 | tf_op jit(solution)/shard_map/all_to_all | solution.py:230
  207.6 2.7 copy-start.15
  210.3 1.2 copy-start.21
  211.5 6.6 %copy-start.18 = (bf16[1,4,64,8,512]{4,3,2,1,0:T(8,128)(2,1)S(1)}, bf16[1,4,64,8,512]{4,3,2,1,0:T(8,128)(2,1)}, u32[]{:S(2)}) copy-start(bf16[1,4,64,8,512]{4,3,2,1,0:T(8,128)(2,1)} %copy-done.17) | copy-start | bytes 6291460
  235.6 33.5 %all-to-all-start.4 = ((bf16[1,2,512,512]{3,1,0,2:T(2,128)(2,1)}), bf16[1,2,512,512]{3,1,0,2:T(2,128)(2,1)}, u32[]{:S(2)}, u32[]{:S(2)}) async-start(bf16[1,2,512,512]{3,1,0,2:T(2,128)(2,1)} %copy.67), calls=%async_computation.4 | async-start | bytes 2097152 | tf_op jit(solution)/shard_map/all_to_all | solution.py:230
  241.1 303.0 %all-reduce.4.cloned.1.call-start = ((), (), s32[]{:S(2)}) async-start(), calls=%async_computation.5 | async-start | bytes 1835008 | tf_op jit(solution)/shard_map/psum | solution.py:254
  272.4 3.7 copy-start.31
  281.8 1.6 copy-start.29
  283.4 1.2 copy-start.16
  284.6 2.8 copy-start.33
  284.6 4.3 copy-start.25
  288.9 4.8 copy-start.42
  288.9 4.7 copy-start.45
  288.9 4.7 copy-start.46
  293.7 256.2 %copy-start.1 = (bf16[128,512]{1,0:T(8,128)(2,1)S(1)}, bf16[128,512]{1,0:T(8,128)(2,1)}, u32[]{:S(2)}) copy-start(bf16[128,512]{1,0:T(8,128)(2,1)} %param.14) | copy-start | bytes 393220
Sparse Core Ops, SparseCore 0:
  288.3 255.7 all-reduce.3
where the time goes:
time: 565 us; the launch traced here: 557 us
  waiting for transfers between devices  254 us (45%)
  blocking collectives  138 us (24%)
  other arithmetic  48.3 us (9%)
  local copies, waits for them, and re-layouts  41.2 us (7%)
  matrix products  37.6 us (7%)
  starting transfers between devices  22.7 us (4%)
  between operations  15.6 us (3%)
    psum x1, waiting for transfers between devices, local(): lax.psum((grad_proj, grad_out, gain_all, bias_all), ('crop', 'row'))  172 us
    psum x1, blocking collectives, local(): lax.psum((grad_proj, grad_out, gain_all, bias_all), ('crop', 'row'))  75.2 us
    all_to_all x1, blocking collectives, side_by_side(): lax.all_to_all(both, axis, split_axis=split_dim, concat_axis=concat_dim,...  62.7 us
    dot_general x17, matrix products, contract(): jnp.einsum(pattern, left_side, right_side, preferred_element_type=jnp.flo...  37.6 us
    all_to_all x2, waiting for transfers between devices, local(): lax.all_to_all(for_sending(channel_grads(grad_owned, left_owned, right_ow...  32.4 us
    all_to_all x1, waiting for transfers between devices, local(): lax.all_to_all(product_owned, 'row', split_axis=2, concat_axis=0, tiled=T...  27 us
    all_to_all x1, waiting for transfers between devices, local(): lax.all_to_all(grad_split, 'row', split_axis=0, concat_axis=2, tiled=True)  22.4 us
    all_to_all x2, starting transfers between devices, local(): lax.all_to_all(for_sending(channel_grads(grad_owned, left_owned, right_ow...  11.6 us
  transfers between devices with their start and end apart: 5, of which 5 were waited for; matrix products, arithmetic and copies ran while one was open for 7% of the time, Pallas kernels for 0%

commit v1 on v0

--- a/solution.py
+++ b/solution.py
@@ -252,7 +252,7 @@
     gain_all = jnp.stack([gain_in, gain_prod, gain_tran])
     bias_all = jnp.stack([bias_in, bias_prod, bias_tran])
     summed_proj, summed_out, summed_gain, summed_bias = lax.psum(
-        (grad_proj, grad_out, gain_all, bias_all), ("crop", "row")
+        lax.psum((grad_proj, grad_out, gain_all, bias_all), "row"), "crop"
     )
     factor = 1.0 / (rows_here * groups)
     return (

time: 565 us -> 1300 us (2.30)
  waiting for transfers between devices: 254 us -> 834 us
  blocking collectives: 138 us -> 294 us
    psum x1 -> x3, waiting for transfers between devices: 172 us -> 792 us  [the longest x1 446 us: local(): lax.psum((grad_proj, grad_out, gain_all, bias_all), 'row')]
    psum x1 -> x2, blocking collectives: 75.2 us -> 198 us  [the longest x1 164 us: local(): lax.psum((grad_proj, grad_out, gain_all, bias_all), 'row')]
    all_to_all x0 -> x1, blocking collectives: none -> 33.1 us  [local(): lax.all_to_all(grad_split, 'row', split_axis=0, concat_axis=2, tiled=True)]
    all_to_all x1 -> x0, waiting for transfers between devices: 22.4 us -> none  [local(): lax.all_to_all(grad_split, 'row', split_axis=0, concat_axis=2, tiled=True)]
    all_to_all x2, waiting for transfers between devices: 32.4 us -> 15.1 us  [local(): lax.all_to_all(for_sending(channel_grads(grad_owned, left_owned, right_ow...]
  transfers between devices with their start and end apart: 5 -> 6, of which waited for: 5 -> 5; matrix products, arithmetic and copies ran while one was open for 7% -> 3% of each run, Pallas kernels for 0% -> 0%
where the time goes in v1:
time: 1300 us; the launch traced here: 1290 us
  waiting for transfers between devices  834 us (64%)
  blocking collectives  294 us (23%)
  other arithmetic  47.7 us (4%)
  local copies, waits for them, and re-layouts  41.3 us (3%)
  matrix products  35.5 us (3%)
  between operations  17.5 us (1%)
  starting transfers between devices  17 us (1%)
    psum x1, waiting for transfers between devices, local(): lax.psum((grad_proj, grad_out, gain_all, bias_all), 'row')  446 us
    psum x1, waiting for transfers between devices, together(): total = lax.psum(vector, axis)  254 us
    psum x1, blocking collectives, local(): lax.psum((grad_proj, grad_out, gain_all, bias_all), 'row')  164 us
    psum x1, waiting for transfers between devices, local(): lax.psum(lax.psum((grad_proj, grad_out, gain_all, bias_all), 'row'), 'crop')  92.7 us
    all_to_all x1, blocking collectives, side_by_side(): lax.all_to_all(both, axis, split_axis=split_dim, concat_axis=concat_dim,...  62.7 us
    dot_general x17, matrix products, contract(): jnp.einsum(pattern, left_side, right_side, preferred_element_type=jnp.flo...  35.5 us
    psum x1, blocking collectives, local(): lax.psum(lax.psum((grad_proj, grad_out, gain_all, bias_all), 'row'), 'crop')  34.1 us
    all_to_all x1, blocking collectives, local(): lax.all_to_all(grad_split, 'row', split_axis=0, concat_axis=2, tiled=True)  33.1 us
  transfers between devices with their start and end apart: 6, of which 5 were waited for; matrix products, arithmetic and copies ran while one was open for 3% of the time, Pallas kernels for 0%

profile of v1, /device:TPU:1, one launch (start us, length us, event | category | flops | bytes accessed | tf_op | source)
XLA Modules:
  0.0 1287.4 jit_solution(14658209645718938657)
XLA Ops:
  8.7 1.5 copy.46
  11.5 1.3 convolution_bitcast_fusion.1
  12.8 1.4 multiply_convert_fusion.11
  14.2 1.9 copy-done.2
  16.1 1.3 reshape.196
  17.3 1.2 reshape.197
  18.8 3.2 pad_maximum_fusion.1
  22.0 1.1 copy.100
  23.2 62.7 %all_to_all.60 = bf16[64,4,8,512]{3,1,2,0:T(4,128)(2,1)S(1)} all-to-all(bf16[64,4,8,512]{3,1,2,0:T(4,128)(2,1)S(1)} %copy.100), channel_id=1, replica_groups=mesh['crop'=4,'row'=64] {'row'}, dimensions={0} | all-to-all | bytes 4194304 | tf_op jit(solution)/shard_map/all_to_all | solution.py:12
  86.3 1.3 copy-done.16
  88.4 2.1 copy.52
  90.5 5.6 all-to-all-start.1
  96.1 1.3 copy.57
  97.4 27.0 %all-to-all-done.1 = bf16[1,2,512,512]{3,1,0,2:T(2,128)(2,1)S(1)} async-done(((bf16[1,2,512,512]{3,1,0,2:T(2,128)(2,1)}), bf16[1,2,512,512]{3,1,0,2:T(2,128)(2,1)S(1)}, u32[]{:S(2)}, u32[]{:S(2)}) %all-to-all-start.1) | async-done | bytes 1048608 | tf_op jit(solution)/shard_map/all_to_all | solution.py:202
  124.4 0.8 fusion.75
  125.3 2.2 copy_bitcast_fusion.2
  127.4 1.4 multiply_reduce_fusion.1
  128.8 2.7 reshape.204
  132.9 2.6 convert_reduce_fusion
  136.5 1.4 fusion.56
  137.9 3.4 multiply_convert_fusion.1
  141.4 3.1 fusion.81
  144.5 2.1 copy.60
  146.7 2.8 fusion.20
  149.6 4.7 multiply_convert_fusion.3
  154.3 1.5 fusion.38
  155.8 1.4 copy-done.7
  157.1 1.7 multiply_convert_fusion.8
  158.9 2.3 reshape.200
  161.1 2.5 copy.62
  163.7 33.1 %all_to_all.61 = bf16[64,2,8,512]{3,1,2,0:T(2,128)(2,1)S(1)} all-to-all(bf16[64,2,8,512]{3,1,2,0:T(2,128)(2,1)S(1)} %copy.62), channel_id=1, replica_groups=mesh['crop'=4,'row'=64] {'row'}, dimensions={0} | all-to-all | bytes 2097152 | tf_op jit(solution)/shard_map/all_to_all | solution.py:229
  196.8 1.0 copy-done.22
  198.5 2.1 copy.64
  200.5 5.8 all-to-all-start.3
  206.4 3.4 convolution_bitcast_fusion.2
  209.8 6.6 convolution_bitcast_fusion
  216.4 0.8 fusion.42
  217.2 2.1 copy.67
  219.3 15.1 %all-to-all-done.3 = bf16[1,2,512,512]{3,1,0,2:T(2,128)(2,1)} async-done(((bf16[1,2,512,512]{3,1,0,2:T(2,128)(2,1)}), bf16[1,2,512,512]{3,1,0,2:T(2,128)(2,1)}, u32[]{:S(2)}, u32[]{:S(2)}) %all-to-all-start.3) | async-done | bytes 1048608 | tf_op jit(solution)/shard_map/all_to_all | solution.py:230
  234.4 5.5 all-to-all-start.4
  240.0 1.8 pad_maximum_fusion.4
  241.9 2.6 convolution_bitcast_fusion.4
  244.5 2.4 reduce_sum.178
  246.9 1.8 convolution_bitcast_fusion.5
  248.6 253.6 %all-reduce.8.cloned.1.call-done = f32[131072]{0:T(1024)} async-done(((f32[131072]{0:T(1024)}), f32[131072]{0:T(1024)}) %all-reduce.8.cloned.1.call-update) | async-done | bytes 524304 | tf_op jit(solution)/shard_map/psum | solution.py:18
  502.2 1.8 fusion.51
  504.0 0.7 mul.346
  504.7 3.3 copy_bitcast_fusion.1
  508.1 3.9 reshape.205
  512.0 3.3 copy_bitcast_fusion
  515.3 3.7 reshape.206
  519.0 5.6 multiply_convert_fusion.7
  524.7 1.6 convolution_bitcast_fusion.3
  526.3 0.8 fusion.50
  527.5 2.8 fusion.29
  530.3 0.7 pad_maximum_fusion.5
  531.2 4.8 fusion.47
  536.0 2.3 copy.81
  538.3 164.1 %all-reduce = (f32[3,128]{1,0:T(4,128)S(1)}, f32[3,128]{1,0:T(4,128)S(1)}) all-reduce(f32[3,128]{1,0:T(4,128)S(1)} %pad_maximum_fusion.6, f32[3,128]{1,0:T(4,128)S(1)} %pad_maximum_fusion.7), channel_id=1, replica_groups=mesh['crop'=4,'row'=64] {'row'}, use_global_device_ids=true, to_apply=%region_20.0 | all-reduce | flops 768 | bytes 6144 | tf_op jit(solution)/shard_map/psum | solution.py:255
  702.5 34.1 %all-reduce.2 = (f32[3,128]{1,0:T(4,128)S(1)}, f32[3,128]{1,0:T(4,128)S(1)}) all-reduce(f32[3,128]{1,0:T(4,128)S(1)} %get-tuple-element.31, f32[3,128]{1,0:T(4,128)S(1)} %get-tuple-element.32), channel_id=1, replica_groups=mesh['crop'=4,'row'=64] {'crop'}, use_global_device_ids=true, to_apply=%region_21.0 | all-reduce | flops 768 | bytes 6144 | tf_op jit(solution)/shard_map/psum | solution.py:254
  736.6 445.7 %all-reduce.10.cloned.1.call-done = (f32[128,640]{1,0:T(8,128)}, f32[128,128]{1,0:T(8,128)}) async-done(((f32[128,640]{1,0:T(8,128)}, f32[128,128]{1,0:T(8,128)}), (f32[128,640]{1,0:T(8,128)}, f32[128,128]{1,0:T(8,128)})) %all-reduce.10.cloned.1.call-update) | async-done | bytes 393232 | tf_op jit(solution)/shard_map/psum | solution.py:255
  1183.5 92.7 %all-reduce.12.cloned.1.call-done = (f32[128,640]{1,0:T(8,128)}, f32[128,128]{1,0:T(8,128)}) async-done(((f32[128,640]{1,0:T(8,128)}, f32[128,128]{1,0:T(8,128)}), (f32[128,640]{1,0:T(8,128)}, f32[128,128]{1,0:T(8,128)})) %all-reduce.12.cloned.1.call-update) | async-done | bytes 393232 | tf_op jit(solution)/shard_map/psum | solution.py:254
  1276.3 1.7 broadcast_multiply_fusion
  1278.0 1.5 broadcast_multiply_fusion.1
  (154 shorter events, 7.6 us)
Async XLA Ops:
  8.0 128.5 %copy-start = (bf16[128,512]{1,0:T(8,128)(2,1)S(1)}, bf16[128,512]{1,0:T(8,128)(2,1)}, u32[]{:S(2)}) copy-start(bf16[128,512]{1,0:T(8,128)(2,1)} %param.14) | copy-start | bytes 393220
  8.7 2.1 copy-start.58
  8.7 2.1 copy-start.59
  8.7 2.7 copy-start.32
  10.5 122.4 %copy-start.24 = (f32[8,512]{1,0:T(8,128)}, f32[8,512]{1,0:T(8,128)S(1)}, u32[]{:S(2)}) copy-start(f32[8,512]{1,0:T(8,128)S(1)} %broadcast_multiply_fusion.11) | copy-start | bytes 49156
  10.8 122.0 %copy-start.29 = (f32[8,512]{1,0:T(8,128)}, f32[8,512]{1,0:T(8,128)S(1)}, u32[]{:S(2)}) copy-start(f32[8,512]{1,0:T(8,128)S(1)} %add_rsqrt_fusion.2) | copy-start | bytes 49156
  11.4 120.2 %copy-start.46 = (f32[128]{0:T(128)}, f32[128]{0:T(128)S(1)}, u32[]{:S(2)}) copy-start(f32[128]{0:T(128)S(1)} %get-tuple-element.64) | copy-start | bytes 1540
  11.4 121.5 %copy-start.43 = (f32[128]{0:T(128)}, f32[128]{0:T(128)S(1)}, u32[]{:S(2)}) copy-start(f32[128]{0:T(128)S(1)} %get-tuple-element.65) | copy-start | bytes 1540
  11.4 121.5 %copy-start.48 = (f32[128]{0:T(128)}, f32[128]{0:T(128)S(1)}, u32[]{:S(2)}) copy-start(f32[128]{0:T(128)S(1)} %get-tuple-element.57) | copy-start | bytes 1540
  11.4 1.4 copy-start.34
  12.8 3.3 copy-start.2
  17.3 1.5 copy-start.14
  86.3 1.3 copy-start.16
  88.4 7.7 copy-start.19
  90.5 33.9 %all-to-all-start.1 = ((bf16[1,2,512,512]{3,1,0,2:T(2,128)(2,1)}), bf16[1,2,512,512]{3,1,0,2:T(2,128)(2,1)S(1)}, u32[]{:S(2)}, u32[]{:S(2)}) async-start(bf16[1,2,512,512]{3,1,0,2:T(2,128)(2,1)} %copy.52), calls=%async_computation.1 | async-start | bytes 2097152 | tf_op jit(solution)/shard_map/all_to_all | solution.py:202
  131.5 1.4 copy-start.3
  132.3 3.1 copy-start.8
  132.9 2.6 copy-start.12
  132.9 3.6 copy-start.41
  132.9 3.6 copy-start.53
  135.8 70.5 %copy-start.27 = (f32[8,512]{1,0:T(8,128)}, f32[8,512]{1,0:T(8,128)S(1)}, u32[]{:S(2)}) copy-start(f32[8,512]{1,0:T(8,128)S(1)} %add_rsqrt_fusion) | copy-start | bytes 49156
  136.5 1.4 copy-start.20
  136.5 1.4 copy-start.60
  137.9 3.5 copy-start.11
  141.4 3.1 copy-start.13
  144.5 2.2 copy-start.42
  146.7 2.8 copy-start.6
  146.7 2.8 copy-start.9
  149.5 4.7 copy-start.36
  149.5 4.7 copy-start.38
  149.5 4.7 copy-start.4
  149.5 4.7 copy-start.47
  154.2 1.5 copy-start.10
  155.7 1.4 copy-start.7
  161.1 36.6 %copy-start.17 = (bf16[1,4,64,8,512]{4,3,2,1,0:T(8,128)(2,1)S(1)}, bf16[1,4,64,8,512]{4,3,2,1,0:T(8,128)(2,1)}, u32[]{:S(2)}) copy-start(bf16[1,4,64,8,512]{4,3,2,1,0:T(8,128)(2,1)} %copy-done.16) | copy-start | bytes 6291460
  198.5 7.9 copy-start.54
  200.5 33.9 %all-to-all-start.3 = ((bf16[1,2,512,512]{3,1,0,2:T(2,128)(2,1)}), bf16[1,2,512,512]{3,1,0,2:T(2,128)(2,1)}, u32[]{:S(2)}, u32[]{:S(2)}) async-start(bf16[1,2,512,512]{3,1,0,2:T(2,128)(2,1)} %copy.64), calls=%async_computation.3 | async-start | bytes 2097152 | tf_op jit(solution)/shard_map/all_to_all | solution.py:230
  206.3 3.5 copy-start.21
  209.8 6.6 copy-start.18
  209.8 6.6 copy-start.23
  234.4 277.6 %all-to-all-start.4 = ((bf16[1,2,512,512]{3,1,0,2:T(2,128)(2,1)}), bf16[1,2,512,512]{3,1,0,2:T(2,128)(2,1)}, u32[]{:S(2)}, u32[]{:S(2)}) async-start(bf16[1,2,512,512]{3,1,0,2:T(2,128)(2,1)} %copy.67), calls=%async_computation.4 | async-start | bytes 2097152 | tf_op jit(solution)/shard_map/all_to_all | solution.py:230
  239.9 262.3 %all-reduce.8.cloned.1.call-start = ((), (), s32[]{:S(2)}) async-start(), calls=%async_computation.5 | async-start | bytes 1048576 | tf_op jit(solution)/shard_map/psum | solution.py:18
  241.8 5.1 copy-start.25
  241.8 5.1 copy-start.30
  241.8 5.1 copy-start.44
  241.8 5.1 copy-start.49
  241.8 940.5 %all-reduce.10.cloned.1.call-start = ((), (), s32[]{:S(2)}) async-start(), calls=%async_computation.6 | async-start | bytes 786432 | tf_op jit(solution)/shard_map/psum | solution.py:255
  515.3 3.7 copy-start.35
  524.6 1.6 copy-start.33
  526.2 1.2 copy-start.15
  526.2 1.2 copy-start.45
  527.5 3.7 copy-start.26
  527.5 3.7 copy-start.28
  527.5 3.7 copy-start.31
  527.5 3.7 copy-start.37
  527.5 3.7 copy-start.39
  531.1 745.2 %all-reduce.12.cloned.1.call-start = ((), (), s32[]{:S(2)}) async-start(), calls=%async_computation.7 | async-start | bytes 786432 | tf_op jit(solution)/shard_map/psum | solution.py:254
  531.2 748.3 %copy-start.1 = (bf16[128,512]{1,0:T(8,128)(2,1)S(1)}, bf16[128,512]{1,0:T(8,128)(2,1)}, u32[]{:S(2)}) copy-start(bf16[128,512]{1,0:T(8,128)(2,1)} %param.14) | copy-start | bytes 393220
  536.0 2.3 copy-start.51
  536.0 2.3 copy-start.52
  536.0 2.3 copy-start.56
  536.0 2.3 copy-start.50
  536.0 2.3 copy-start.55
  536.0 2.3 copy-start.57
  (3 other events, 2.8 us)
Sparse Core Ops, SparseCore 0:
  246.2 255.9 all-reduce.7
Sparse Core Ops, SparseCore 1:
  531.2 651.1 all-reduce.9
  1184.9 91.3 all-reduce.11
